TPU v7x, 512 devices: a whole 4x4x16 slice. The times are simulated.
512 devices in a mesh: gx: 32 (over y, x, core), gy: 16 (over z).
Axes of the slice: x: 4, y: 4, z: 16, core: 2. Of those that a mesh axis runs over, the one named last changes fastest.
Arguments:
- snapshots: bfloat16 [131072, 2048], P(('gx', 'gy')), may hold values from -6 to 6
- volume: bfloat16 [65536, 2048], P('gx', 'gy'), may hold values from -6 to 6
- start_basis: bfloat16 [64, 131072], P(None, ('gx', 'gy')), may hold values from -6 to 6
- wake_mask: int32 [2048], P(('gx', 'gy')), may hold values 0 or 1
Outputs:
- plane_modes: float32 [64, 131072], P(None, ('gx', 'gy'))
- wake_modes: float32 [64, 65536], P(None, ('gx', 'gy'))
All inputs are finite; a program needn't handle non-finite values. No bound on the sum of `wake_mask` on one device may be relied on, other than what follows from the above.
Results may differ from a plain program's by a relative error of at most 0.018.
Values may be sent and summed in bfloat16 or wider, within the bound.
No kernel may reach another device: no remote copies, remote signals or barrier semaphores. Data moves between devices by JAX's collectives and lax.ppermute only.
A program may use at most 64 MiB of HBM per device.

v0:
```python
import jax
import jax.numpy as jnp
from jax import lax
from jax.sharding import Mesh
from jax.sharding import PartitionSpec as P

ITERS = 3
CBLOCK = 32
GX_GY = ("gx_0", "gx_1", "gx_2", "gy")
GX = ("gx_0", "gx_1", "gx_2")


def one_axis_at_a_time(array, axes):
    for axis in axes:
        array = lax.psum(array, axis)
    return array


def cut_along(array, dim, count):
    lengths = array.shape
    tiles = array.reshape(*lengths[:dim], count, lengths[dim] // count, *lengths[dim + 1 :])
    return jnp.moveaxis(tiles, dim, 0)


def sent_and_summed(array, axis, dim):
    tiles = cut_along(array, dim, lax.axis_size(axis))
    arrived = lax.all_to_all(tiles, axis, split_axis=0, concat_axis=0, tiled=True)
    return arrived.sum(axis=0)


def summed_rows(array, axes, dim):
    far, near = axes
    tiles = cut_along(array, dim, lax.axis_size(far))
    nearer = sent_and_summed(tiles, near, dim + 1)
    arrived = lax.all_to_all(nearer, far, split_axis=0, concat_axis=0, tiled=True)
    return arrived.sum(axis=0)


def filled_up(lines, count):
    spare = -len(lines) % count
    return jnp.pad(lines, [(0, spare)] + [(0, 0)] * (lines.ndim - 1))


def copy_for_each(array, axis):
    copies = jnp.broadcast_to(array, (lax.axis_size(axis), *array.shape))
    return lax.all_to_all(copies, axis, split_axis=0, concat_axis=0, tiled=True)


def laid_out(tiles, dim):
    tiles = jnp.moveaxis(tiles, 0, dim)
    lengths = tiles.shape
    return tiles.reshape(*lengths[:dim], lengths[dim] * lengths[dim + 1], *lengths[dim + 2 :])


def gather_axes(array, axes, dim):
    far, near = axes
    tiles = copy_for_each(copy_for_each(array, far), near)
    return laid_out(tiles.swapaxes(0, 1).reshape(-1, *array.shape), dim)


def sum_by_parts(array, axes):
    lines = array.reshape(-1)
    own = summed_rows(filled_up(lines, lax.axis_size(axes[0]) * lax.axis_size(axes[1])), axes, 0)
    whole = gather_axes(own, axes, 0)
    return whole[: len(lines)].reshape(array.shape)


def triangular(lower, right):
    return jax.scipy.linalg.solve_triangular(lower, right, lower=True)


def temporal_weights(basis, snapshots):
    gram_part = jnp.dot(basis, basis.T, preferred_element_type=jnp.float32)
    coeff_part = jnp.dot(basis, snapshots, preferred_element_type=jnp.float32)
    gram = one_axis_at_a_time(gram_part, GX_GY)
    lower = jnp.linalg.cholesky(gram)
    weights = sum_by_parts(triangular(lower, coeff_part), (("gx_0", "gx_1"), ("gx_2", "gy")))
    return (lower, weights)


def local(snapshots, volume, start_basis, wake_mask):
    basis = start_basis
    for step in range(ITERS):
        lower, weights = temporal_weights(basis, snapshots)
        weights_b = weights.astype(jnp.bfloat16)
        basis = lax.dot_general(
            weights_b, snapshots, (((1,), (1,)), ((), ())), preferred_element_type=jnp.float32
        ).astype(jnp.bfloat16)
    lower, weights = temporal_weights(basis, snapshots)
    total_points = snapshots.shape[0] * lax.axis_size(GX) * lax.axis_size("gy")
    plane_modes = triangular(lower, basis.astype(jnp.float32)) * jnp.sqrt(jnp.float32(total_points))
    norms = jnp.sqrt(jnp.sum(weights * weights, axis=1, keepdims=True))
    scaled = (weights / norms).astype(jnp.bfloat16)
    own_cells = lax.all_to_all(volume, "gy", split_axis=0, concat_axis=1, tiled=True)
    projection = lax.dot_general(
        scaled, own_cells, (((1,), (1,)), ((), ())), preferred_element_type=jnp.float32
    )
    cell_mask = jnp.repeat(wake_mask, CBLOCK).astype(jnp.float32)
    return (plane_modes, projection * cell_mask[None, :])


def solution(mesh):
    finer = Mesh(mesh.devices.reshape(4, 4, 2, mesh.shape["gy"]), ("gx_0", "gx_1", "gx_2", "gy"))
    placed = (P(GX_GY, None), P(GX, "gy"), P(None, GX_GY), P(GX_GY))
    return jax.shard_map(
        local,
        mesh=finer,
        in_specs=placed,
        out_specs=(P(None, GX_GY), P(None, GX_GY)),
        check_vma=False,
    )
```

profile of v0, /device:TPU:33, one launch (start us, length us, event | category | flops | bytes accessed | tf_op | source)
XLA Modules:
  0.0 810.4 jit_solution(11774204600463809200)
XLA Ops:
  1.6 13.6 %psum.112 = f32[64,64]{0,1:T(8,128)S(1)} all-reduce(f32[64,64]{0,1:T(8,128)S(1)} %fusion.25), channel_id=1, replica_groups=mesh['gx_0'=4,'gx_1'=4,'gx_2'=2,'gy'=16] {'gx_0'}, use_global_device_ids=true, to_apply=%region_0.0 | all-reduce | flops 4096 | bytes 32768 | tf_op jit(solution)/shard_map/psum | solution.py:15
  15.2 13.3 %psum.113 = f32[64,64]{0,1:T(8,128)S(1)} all-reduce(f32[64,64]{0,1:T(8,128)S(1)} %psum.112), channel_id=1, replica_groups=mesh['gx_0'=4,'gx_1'=4,'gx_2'=2,'gy'=16] {'gx_1'}, use_global_device_ids=true, to_apply=%region_1.0 | all-reduce | flops 4096 | bytes 32768 | tf_op jit(solution)/shard_map/psum | solution.py:15
  28.5 11.4 %psum.114 = f32[64,64]{0,1:T(8,128)S(1)} all-reduce(f32[64,64]{0,1:T(8,128)S(1)} %psum.113), channel_id=1, replica_groups=mesh['gx_0'=4,'gx_1'=4,'gx_2'=2,'gy'=16] {'gx_2'}, use_global_device_ids=true, to_apply=%region_2.0 | all-reduce | flops 4096 | bytes 32768 | tf_op jit(solution)/shard_map/psum | solution.py:15
  40.0 45.1 %psum.115 = f32[64,64]{0,1:T(8,128)S(1)} all-reduce(f32[64,64]{0,1:T(8,128)S(1)} %psum.114), channel_id=1, replica_groups=mesh['gx_0'=4,'gx_1'=4,'gx_2'=2,'gy'=16] {'gy'}, use_global_device_ids=true, to_apply=%region_3.0 | all-reduce | flops 4096 | bytes 32768 | tf_op jit(solution)/shard_map/psum | solution.py:15
  98.6 55.1 %all_to_all.131 = f32[32,16,256]{2,1,0:T(8,128)S(1)} all-to-all(f32[32,16,256]{2,1,0:T(8,128)S(1)} %bitcast.116), channel_id=1, replica_groups=mesh['gx_0'=4,'gx_1'=4,'gx_2'=2,'gy'=16] {'gx_2','gy'}, dimensions={0} | all-to-all | bytes 1048576 | tf_op jit(solution)/shard_map/all_to_all | solution.py:27
  174.2 27.7 %all_to_all.134 = bf16[32,16,256]{2,1,0:T(8,128)(2,1)S(1)} all-to-all(bf16[32,16,256]{2,1,0:T(8,128)(2,1)S(1)} %broadcast_in_dim.31), channel_id=1, replica_groups=mesh['gx_0'=4,'gx_1'=4,'gx_2'=2,'gy'=16] {'gx_2','gy'}, dimensions={0} | all-to-all | bytes 524288 | tf_op jit(solution)/shard_map/all_to_all | solution.py:46
  203.0 11.7 %psum.116 = f32[64,64]{0,1:T(8,128)S(1)} all-reduce(f32[64,64]{0,1:T(8,128)S(1)} %fusion.27), channel_id=1, replica_groups=mesh['gx_0'=4,'gx_1'=4,'gx_2'=2,'gy'=16] {'gx_0'}, use_global_device_ids=true, to_apply=%region_8.11 | all-reduce | flops 4096 | bytes 32768 | tf_op jit(solution)/shard_map/psum | solution.py:15
  214.7 11.7 %psum.117 = f32[64,64]{0,1:T(8,128)S(1)} all-reduce(f32[64,64]{0,1:T(8,128)S(1)} %psum.116), channel_id=1, replica_groups=mesh['gx_0'=4,'gx_1'=4,'gx_2'=2,'gy'=16] {'gx_1'}, use_global_device_ids=true, to_apply=%region_9.12 | all-reduce | flops 4096 | bytes 32768 | tf_op jit(solution)/shard_map/psum | solution.py:15
  226.5 10.5 %psum.118 = f32[64,64]{0,1:T(8,128)S(1)} all-reduce(f32[64,64]{0,1:T(8,128)S(1)} %psum.117), channel_id=1, replica_groups=mesh['gx_0'=4,'gx_1'=4,'gx_2'=2,'gy'=16] {'gx_2'}, use_global_device_ids=true, to_apply=%region_10.13 | all-reduce | flops 4096 | bytes 32768 | tf_op jit(solution)/shard_map/psum | solution.py:15
  237.0 38.3 %psum.119 = f32[64,64]{0,1:T(8,128)S(1)} all-reduce(f32[64,64]{0,1:T(8,128)S(1)} %psum.118), channel_id=1, replica_groups=mesh['gx_0'=4,'gx_1'=4,'gx_2'=2,'gy'=16] {'gy'}, use_global_device_ids=true, to_apply=%region_11.14 | all-reduce | flops 4096 | bytes 32768 | tf_op jit(solution)/shard_map/psum | solution.py:15
  288.5 53.1 %all_to_all.135 = f32[32,16,256]{2,1,0:T(8,128)S(1)} all-to-all(f32[32,16,256]{2,1,0:T(8,128)S(1)} %bitcast.117), channel_id=1, replica_groups=mesh['gx_0'=4,'gx_1'=4,'gx_2'=2,'gy'=16] {'gx_2','gy'}, dimensions={0} | all-to-all | bytes 1048576 | tf_op jit(solution)/shard_map/all_to_all | solution.py:27
  361.6 27.8 %all_to_all.138 = bf16[32,16,256]{2,1,0:T(8,128)(2,1)S(1)} all-to-all(bf16[32,16,256]{2,1,0:T(8,128)(2,1)S(1)} %broadcast_in_dim.33), channel_id=1, replica_groups=mesh['gx_0'=4,'gx_1'=4,'gx_2'=2,'gy'=16] {'gx_2','gy'}, dimensions={0} | all-to-all | bytes 524288 | tf_op jit(solution)/shard_map/all_to_all | solution.py:46
  390.5 11.7 %psum.120 = f32[64,64]{0,1:T(8,128)S(1)} all-reduce(f32[64,64]{0,1:T(8,128)S(1)} %fusion.29), channel_id=1, replica_groups=mesh['gx_0'=4,'gx_1'=4,'gx_2'=2,'gy'=16] {'gx_0'}, use_global_device_ids=true, to_apply=%region_14.17 | all-reduce | flops 4096 | bytes 32768 | tf_op jit(solution)/shard_map/psum | solution.py:15
  402.2 11.7 %psum.121 = f32[64,64]{0,1:T(8,128)S(1)} all-reduce(f32[64,64]{0,1:T(8,128)S(1)} %psum.120), channel_id=1, replica_groups=mesh['gx_0'=4,'gx_1'=4,'gx_2'=2,'gy'=16] {'gx_1'}, use_global_device_ids=true, to_apply=%region_15.18 | all-reduce | flops 4096 | bytes 32768 | tf_op jit(solution)/shard_map/psum | solution.py:15
  424.4 38.9 %psum.123 = f32[64,64]{0,1:T(8,128)S(1)} all-reduce(f32[64,64]{0,1:T(8,128)S(1)} %psum.122), channel_id=1, replica_groups=mesh['gx_0'=4,'gx_1'=4,'gx_2'=2,'gy'=16] {'gy'}, use_global_device_ids=true, to_apply=%region_17.20 | all-reduce | flops 4096 | bytes 32768 | tf_op jit(solution)/shard_map/psum | solution.py:15
  476.5 52.5 %all_to_all.139 = f32[32,16,256]{2,1,0:T(8,128)S(1)} all-to-all(f32[32,16,256]{2,1,0:T(8,128)S(1)} %bitcast.118), channel_id=1, replica_groups=mesh['gx_0'=4,'gx_1'=4,'gx_2'=2,'gy'=16] {'gx_2','gy'}, dimensions={0} | all-to-all | bytes 1048576 | tf_op jit(solution)/shard_map/all_to_all | solution.py:27
  549.0 27.7 %all_to_all.142 = bf16[32,16,256]{2,1,0:T(8,128)(2,1)S(1)} all-to-all(bf16[32,16,256]{2,1,0:T(8,128)(2,1)S(1)} %broadcast_in_dim.35), channel_id=1, replica_groups=mesh['gx_0'=4,'gx_1'=4,'gx_2'=2,'gy'=16] {'gx_2','gy'}, dimensions={0} | all-to-all | bytes 524288 | tf_op jit(solution)/shard_map/all_to_all | solution.py:46
  577.9 11.7 %psum.124 = f32[64,64]{0,1:T(8,128)S(1)} all-reduce(f32[64,64]{0,1:T(8,128)S(1)} %fusion.31), channel_id=1, replica_groups=mesh['gx_0'=4,'gx_1'=4,'gx_2'=2,'gy'=16] {'gx_0'}, use_global_device_ids=true, to_apply=%region_20.23 | all-reduce | flops 4096 | bytes 32768 | tf_op jit(solution)/shard_map/psum | solution.py:15
  589.6 11.7 %psum.125 = f32[64,64]{0,1:T(8,128)S(1)} all-reduce(f32[64,64]{0,1:T(8,128)S(1)} %psum.124), channel_id=1, replica_groups=mesh['gx_0'=4,'gx_1'=4,'gx_2'=2,'gy'=16] {'gx_1'}, use_global_device_ids=true, to_apply=%region_21.24 | all-reduce | flops 4096 | bytes 32768 | tf_op jit(solution)/shard_map/psum | solution.py:15
  611.9 38.3 %psum.127 = f32[64,64]{0,1:T(8,128)S(1)} all-reduce(f32[64,64]{0,1:T(8,128)S(1)} %psum.126), channel_id=1, replica_groups=mesh['gx_0'=4,'gx_1'=4,'gx_2'=2,'gy'=16] {'gy'}, use_global_device_ids=true, to_apply=%region_23.26 | all-reduce | flops 4096 | bytes 32768 | tf_op jit(solution)/shard_map/psum | solution.py:15
  663.4 53.1 %all_to_all.143 = f32[32,16,256]{2,1,0:T(8,128)S(1)} all-to-all(f32[32,16,256]{2,1,0:T(8,128)S(1)} %bitcast.119), channel_id=1, replica_groups=mesh['gx_0'=4,'gx_1'=4,'gx_2'=2,'gy'=16] {'gx_2','gy'}, dimensions={0} | all-to-all | bytes 1048576 | tf_op jit(solution)/shard_map/all_to_all | solution.py:27
  739.6 23.8 %all-to-all-done.16 = bf16[16,128,128]{2,1,0:T(8,128)(2,1)S(1)} async-done(((bf16[16,128,128]{2,1,0:T(8,128)(2,1)}), bf16[16,128,128]{2,1,0:T(8,128)(2,1)S(1)}, u32[]{:S(2)}, u32[]{:S(2)}) %all-to-all-start.16) | async-done | bytes 524320 | tf_op jit(solution)/shard_map/all_to_all | solution.py:94
  764.2 12.7 %all-to-all-start.15 = ((f32[32,16,256]{2,1,0:T(8,128)}), f32[32,16,256]{2,1,0:T(8,128)S(1)}, u32[]{:S(2)}, u32[]{:S(2)}) async-start(f32[32,16,256]{2,1,0:T(8,128)} %broadcast_in_dim.37), calls=%async_computation.15 | async-start | bytes 1048576 | tf_op jit(solution)/shard_map/all_to_all | solution.py:46
  778.2 30.3 %all-to-all-done.15 = f32[32,16,256]{2,1,0:T(8,128)S(1)} async-done(((f32[32,16,256]{2,1,0:T(8,128)}), f32[32,16,256]{2,1,0:T(8,128)S(1)}, u32[]{:S(2)}, u32[]{:S(2)}) %all-to-all-start.15) | async-done | bytes 524320 | tf_op jit(solution)/shard_map/all_to_all | solution.py:46
  (125 shorter events, 165.8 us)
Async XLA Ops:
  0.6 96.6 %copy-start = (bf16[256,2048]{1,0:T(8,128)(2,1)S(1)}, bf16[256,2048]{1,0:T(8,128)(2,1)}, u32[]{:S(2)}) copy-start(bf16[256,2048]{1,0:T(8,128)(2,1)} %param.7) | copy-start | bytes 3145732
  91.7 5.6 copy-start.1
  735.7 27.6 %all-to-all-start.16 = ((bf16[16,128,128]{2,1,0:T(8,128)(2,1)}), bf16[16,128,128]{2,1,0:T(8,128)(2,1)S(1)}, u32[]{:S(2)}, u32[]{:S(2)}) async-start(bf16[16,128,128]{2,1,0:T(8,128)(2,1)} %bitcast.23), calls=%async_computation.16 | async-start | bytes 1048576 | tf_op jit(solution)/shard_map/all_to_all | solution.py:94
  764.2 12.7 %copy-start.2 = (s32[4]{0:T(128)S(1)}, s32[4]{0:T(128)}, u32[]{:S(2)}) copy-start(s32[4]{0:T(128)} %param.10) | copy-start | bytes 52
  764.2 44.3 %all-to-all-start.15 = ((f32[32,16,256]{2,1,0:T(8,128)}), f32[32,16,256]{2,1,0:T(8,128)S(1)}, u32[]{:S(2)}, u32[]{:S(2)}) async-start(f32[32,16,256]{2,1,0:T(8,128)} %broadcast_in_dim.37), calls=%async_computation.15 | async-start | bytes 1048576 | tf_op jit(solution)/shard_map/all_to_all | solution.py:46
where the time goes:
time: 812 us; the launch traced here: 810 us
  blocking collectives  674 us (83%)
  waiting for transfers between devices  54.1 us (7%)
  other arithmetic  51.2 us (6%)
  starting transfers between devices  16.6 us (2%)
  matrix products  8.18 us (1%)
    psum x16, blocking collectives, one_axis_at_a_time(): array = lax.psum(array, axis)  301 us
    all_to_all x4, blocking collectives, sent_and_summed(): lax.all_to_all(tiles, axis, split_axis=0, concat_axis=0, tiled=True)  214 us
    all_to_all x7, blocking collectives, copy_for_each(): return lax.all_to_all(copies, axis, split_axis=0, concat_axis=0, tiled=True)  121 us
    all_to_all x4, blocking collectives, summed_rows(): lax.all_to_all(nearer, far, split_axis=0, concat_axis=0, tiled=True)  38.6 us
    all_to_all x1, waiting for transfers between devices, copy_for_each(): return lax.all_to_all(copies, axis, split_axis=0, concat_axis=0, tiled=True)  30.3 us
    another operation x12, other arithmetic, temporal_weights(): lower = jnp.linalg.cholesky(gram)  26.1 us
    all_to_all x1, waiting for transfers between devices, local(): lax.all_to_all(volume, 'gy', split_axis=0, concat_axis=1, tiled=True)  23.8 us
    another operation x8, other arithmetic, triangular(): return jax.scipy.linalg.solve_triangular(lower, right, lower=True)  22.2 us
  transfers between devices with their start and end apart: 2, of which 2 were waited for; matrix products, arithmetic and copies ran while one was open for 0% of the time, Pallas kernels for 0%

commit v1 on v0

--- a/solution.py
+++ b/solution.py
@@ -12,7 +12,8 @@
 
 def one_axis_at_a_time(array, axes):
     for axis in axes:
-        array = lax.psum(array, axis)
+        blocks = lax.all_gather(array, axis)
+        array = jnp.sum(blocks, axis=0)
     return array
 
 

time: 812 us -> 682 us (0.84)
  blocking collectives: 674 us -> 545 us
    psum x16 -> x0, blocking collectives: 301 us -> none  [one_axis_at_a_time(): array = lax.psum(array, axis)]
    all_gather x0 -> x16, blocking collectives: none -> 201 us  [one_axis_at_a_time(): blocks = lax.all_gather(array, axis)]
    all_to_all x4, blocking collectives: 214 us -> 182 us  [sent_and_summed(): lax.all_to_all(tiles, axis, split_axis=0, concat_axis=0, tiled=True)]
where the time goes in v1:
time: 682 us; the launch traced here: 681 us
  blocking collectives  545 us (80%)
  waiting for transfers between devices  54.1 us (8%)
  other arithmetic  51.5 us (8%)
  starting transfers between devices  16.6 us (2%)
  matrix products  8.19 us (1%)
    all_gather x16, blocking collectives, one_axis_at_a_time(): blocks = lax.all_gather(array, axis)  201 us
    all_to_all x4, blocking collectives, sent_and_summed(): lax.all_to_all(tiles, axis, split_axis=0, concat_axis=0, tiled=True)  182 us
    all_to_all x7, blocking collectives, copy_for_each(): return lax.all_to_all(copies, axis, split_axis=0, concat_axis=0, tiled=True)  121 us
    all_to_all x4, blocking collectives, summed_rows(): lax.all_to_all(nearer, far, split_axis=0, concat_axis=0, tiled=True)  40.8 us
    all_to_all x1, waiting for transfers between devices, copy_for_each(): return lax.all_to_all(copies, axis, split_axis=0, concat_axis=0, tiled=True)  30.3 us
    another operation x12, other arithmetic, temporal_weights(): lower = jnp.linalg.cholesky(gram)  26.1 us
    all_to_all x1, waiting for transfers between devices, local(): lax.all_to_all(volume, 'gy', split_axis=0, concat_axis=1, tiled=True)  23.8 us
    another operation x8, other arithmetic, triangular(): return jax.scipy.linalg.solve_triangular(lower, right, lower=True)  22.2 us
  transfers between devices with their start and end apart: 2, of which 2 were waited for; matrix products, arithmetic and copies ran while one was open for 0% of the time, Pallas kernels for 0%

profile of v1, /device:TPU:33, one launch (start us, length us, event | category | flops | bytes accessed | tf_op | source)
XLA Modules:
  0.0 681.1 jit_solution(10981907031086914121)
XLA Ops:
  1.6 9.7 %all-gather = f32[256,64]{1,0:T(8,128)S(1)} all-gather(f32[64,64]{1,0:T(8,128)S(1)} %fusion.25), channel_id=2, replica_groups=mesh['gx_0'=4,'gx_1'=4,'gx_2'=2,'gy'=16] {'gx_0'}, dimensions={0}, use_global_device_ids=true | all-gather | bytes 81920 | tf_op jit(solution)/shard_map/all_gather | solution.py:15
  11.4 9.5 %all-gather.1 = f32[256,64]{1,0:T(8,128)S(1)} all-gather(f32[64,64]{1,0:T(8,128)S(1)} %reduce_sum.232), channel_id=3, replica_groups=mesh['gx_0'=4,'gx_1'=4,'gx_2'=2,'gy'=16] {'gx_1'}, dimensions={0}, use_global_device_ids=true | all-gather | bytes 81920 | tf_op jit(solution)/shard_map/all_gather | solution.py:15
  28.7 29.4 %all-gather.3 = f32[1024,64]{1,0:T(8,128)S(1)} all-gather(f32[64,64]{1,0:T(8,128)S(1)} %reduce_sum.234), channel_id=5, replica_groups=mesh['gx_0'=4,'gx_1'=4,'gx_2'=2,'gy'=16] {'gy'}, dimensions={0}, use_global_device_ids=true | all-gather | bytes 278528 | tf_op jit(solution)/shard_map/all_gather | solution.py:15
  71.8 47.5 %all_to_all.131 = f32[32,16,256]{2,1,0:T(8,128)S(1)} all-to-all(f32[32,16,256]{2,1,0:T(8,128)S(1)} %bitcast.136), channel_id=1, replica_groups=mesh['gx_0'=4,'gx_1'=4,'gx_2'=2,'gy'=16] {'gx_2','gy'}, dimensions={0} | all-to-all | bytes 1048576 | tf_op jit(solution)/shard_map/all_to_all | solution.py:28
  119.3 11.7 %all_to_all.132 = f32[16,1,256]{2,1,0:T(1,128)S(1)} all-to-all(f32[16,1,256]{2,1,0:T(1,128)S(1)} %all_to_all.87), channel_id=1, replica_groups=mesh['gx_0'=4,'gx_1'=4,'gx_2'=2,'gy'=16] {'gx_0','gx_1'}, dimensions={0} | all-to-all | bytes 32768 | tf_op jit(solution)/shard_map/all_to_all | solution.py:36
  132.3 9.5 %all_to_all.133 = bf16[16,2,128]{2,1,0:T(2,128)(2,1)S(1)} all-to-all(bf16[16,2,128]{2,1,0:T(2,128)(2,1)S(1)} %reshape.88), channel_id=1, replica_groups=mesh['gx_0'=4,'gx_1'=4,'gx_2'=2,'gy'=16] {'gx_0','gx_1'}, dimensions={0} | all-to-all | bytes 16384 | tf_op jit(solution)/shard_map/all_to_all | solution.py:47
  141.8 27.7 %all_to_all.134 = bf16[32,16,256]{2,1,0:T(8,128)(2,1)S(1)} all-to-all(bf16[32,16,256]{2,1,0:T(8,128)(2,1)S(1)} %broadcast_in_dim.31), channel_id=1, replica_groups=mesh['gx_0'=4,'gx_1'=4,'gx_2'=2,'gy'=16] {'gx_2','gy'}, dimensions={0} | all-to-all | bytes 524288 | tf_op jit(solution)/shard_map/all_to_all | solution.py:47
  195.9 22.8 %all-gather.7 = f32[1024,64]{1,0:T(8,128)S(1)} all-gather(f32[64,64]{1,0:T(8,128)S(1)} %reduce_sum.240), channel_id=9, replica_groups=mesh['gx_0'=4,'gx_1'=4,'gx_2'=2,'gy'=16] {'gy'}, dimensions={0}, use_global_device_ids=true | all-gather | bytes 278528 | tf_op jit(solution)/shard_map/all_gather | solution.py:15
  232.0 44.8 %all_to_all.135 = f32[32,16,256]{2,1,0:T(8,128)S(1)} all-to-all(f32[32,16,256]{2,1,0:T(8,128)S(1)} %bitcast.137), channel_id=1, replica_groups=mesh['gx_0'=4,'gx_1'=4,'gx_2'=2,'gy'=16] {'gx_2','gy'}, dimensions={0} | all-to-all | bytes 1048576 | tf_op jit(solution)/shard_map/all_to_all | solution.py:28
  276.9 9.7 %all_to_all.136 = f32[16,1,256]{2,1,0:T(1,128)S(1)} all-to-all(f32[16,1,256]{2,1,0:T(1,128)S(1)} %all_to_all.93), channel_id=1, replica_groups=mesh['gx_0'=4,'gx_1'=4,'gx_2'=2,'gy'=16] {'gx_0','gx_1'}, dimensions={0} | all-to-all | bytes 32768 | tf_op jit(solution)/shard_map/all_to_all | solution.py:36
  287.4 9.5 %all_to_all.137 = bf16[16,2,128]{2,1,0:T(2,128)(2,1)S(1)} all-to-all(bf16[16,2,128]{2,1,0:T(2,128)(2,1)S(1)} %reshape.90), channel_id=1, replica_groups=mesh['gx_0'=4,'gx_1'=4,'gx_2'=2,'gy'=16] {'gx_0','gx_1'}, dimensions={0} | all-to-all | bytes 16384 | tf_op jit(solution)/shard_map/all_to_all | solution.py:47
  296.9 27.7 %all_to_all.138 = bf16[32,16,256]{2,1,0:T(8,128)(2,1)S(1)} all-to-all(bf16[32,16,256]{2,1,0:T(8,128)(2,1)S(1)} %broadcast_in_dim.33), channel_id=1, replica_groups=mesh['gx_0'=4,'gx_1'=4,'gx_2'=2,'gy'=16] {'gx_2','gy'}, dimensions={0} | all-to-all | bytes 524288 | tf_op jit(solution)/shard_map/all_to_all | solution.py:47
  351.0 23.0 %all-gather.11 = f32[1024,64]{1,0:T(8,128)S(1)} all-gather(f32[64,64]{1,0:T(8,128)S(1)} %reduce_sum.246), channel_id=13, replica_groups=mesh['gx_0'=4,'gx_1'=4,'gx_2'=2,'gy'=16] {'gy'}, dimensions={0}, use_global_device_ids=true | all-gather | bytes 278528 | tf_op jit(solution)/shard_map/all_gather | solution.py:15
  387.3 44.8 %all_to_all.139 = f32[32,16,256]{2,1,0:T(8,128)S(1)} all-to-all(f32[32,16,256]{2,1,0:T(8,128)S(1)} %bitcast.138), channel_id=1, replica_groups=mesh['gx_0'=4,'gx_1'=4,'gx_2'=2,'gy'=16] {'gx_2','gy'}, dimensions={0} | all-to-all | bytes 1048576 | tf_op jit(solution)/shard_map/all_to_all | solution.py:28
  432.2 9.7 %all_to_all.140 = f32[16,1,256]{2,1,0:T(1,128)S(1)} all-to-all(f32[16,1,256]{2,1,0:T(1,128)S(1)} %all_to_all.99), channel_id=1, replica_groups=mesh['gx_0'=4,'gx_1'=4,'gx_2'=2,'gy'=16] {'gx_0','gx_1'}, dimensions={0} | all-to-all | bytes 32768 | tf_op jit(solution)/shard_map/all_to_all | solution.py:36
  442.6 9.5 %all_to_all.141 = bf16[16,2,128]{2,1,0:T(2,128)(2,1)S(1)} all-to-all(bf16[16,2,128]{2,1,0:T(2,128)(2,1)S(1)} %reshape.92), channel_id=1, replica_groups=mesh['gx_0'=4,'gx_1'=4,'gx_2'=2,'gy'=16] {'gx_0','gx_1'}, dimensions={0} | all-to-all | bytes 16384 | tf_op jit(solution)/shard_map/all_to_all | solution.py:47
  452.1 27.7 %all_to_all.142 = bf16[32,16,256]{2,1,0:T(8,128)(2,1)S(1)} all-to-all(bf16[32,16,256]{2,1,0:T(8,128)(2,1)S(1)} %broadcast_in_dim.35), channel_id=1, replica_groups=mesh['gx_0'=4,'gx_1'=4,'gx_2'=2,'gy'=16] {'gx_2','gy'}, dimensions={0} | all-to-all | bytes 524288 | tf_op jit(solution)/shard_map/all_to_all | solution.py:47
  506.3 22.8 %all-gather.15 = f32[1024,64]{1,0:T(8,128)S(1)} all-gather(f32[64,64]{1,0:T(8,128)S(1)} %reduce_sum.252), channel_id=17, replica_groups=mesh['gx_0'=4,'gx_1'=4,'gx_2'=2,'gy'=16] {'gy'}, dimensions={0}, use_global_device_ids=true | all-gather | bytes 278528 | tf_op jit(solution)/shard_map/all_gather | solution.py:15
  542.4 44.8 %all_to_all.143 = f32[32,16,256]{2,1,0:T(8,128)S(1)} all-to-all(f32[32,16,256]{2,1,0:T(8,128)S(1)} %bitcast.139), channel_id=1, replica_groups=mesh['gx_0'=4,'gx_1'=4,'gx_2'=2,'gy'=16] {'gx_2','gy'}, dimensions={0} | all-to-all | bytes 1048576 | tf_op jit(solution)/shard_map/all_to_all | solution.py:28
  587.3 9.7 %all_to_all.144 = f32[16,1,256]{2,1,0:T(1,128)S(1)} all-to-all(f32[16,1,256]{2,1,0:T(1,128)S(1)} %all_to_all.105), channel_id=1, replica_groups=mesh['gx_0'=4,'gx_1'=4,'gx_2'=2,'gy'=16] {'gx_0','gx_1'}, dimensions={0} | all-to-all | bytes 32768 | tf_op jit(solution)/shard_map/all_to_all | solution.py:36
  597.0 9.5 %all_to_all.145 = f32[16,1,256]{2,1,0:T(1,128)S(1)} all-to-all(f32[16,1,256]{2,1,0:T(1,128)S(1)} %broadcast_in_dim.36), channel_id=1, replica_groups=mesh['gx_0'=4,'gx_1'=4,'gx_2'=2,'gy'=16] {'gx_0','gx_1'}, dimensions={0} | all-to-all | bytes 32768 | tf_op jit(solution)/shard_map/all_to_all | solution.py:47
  610.3 23.8 %all-to-all-done.16 = bf16[16,128,128]{2,1,0:T(8,128)(2,1)S(1)} async-done(((bf16[16,128,128]{2,1,0:T(8,128)(2,1)}), bf16[16,128,128]{2,1,0:T(8,128)(2,1)S(1)}, u32[]{:S(2)}, u32[]{:S(2)}) %all-to-all-start.16) | async-done | bytes 524320 | tf_op jit(solution)/shard_map/all_to_all | solution.py:95
  635.0 12.7 %all-to-all-start.15 = ((f32[32,16,256]{2,1,0:T(8,128)}), f32[32,16,256]{2,1,0:T(8,128)S(1)}, u32[]{:S(2)}, u32[]{:S(2)}) async-start(f32[32,16,256]{2,1,0:T(8,128)} %broadcast_in_dim.37), calls=%async_computation.15 | async-start | bytes 1048576 | tf_op jit(solution)/shard_map/all_to_all | solution.py:47
  649.0 30.3 %all-to-all-done.15 = f32[32,16,256]{2,1,0:T(8,128)S(1)} async-done(((f32[32,16,256]{2,1,0:T(8,128)}), f32[32,16,256]{2,1,0:T(8,128)S(1)}, u32[]{:S(2)}, u32[]{:S(2)}) %all-to-all-start.15) | async-done | bytes 524320 | tf_op jit(solution)/shard_map/all_to_all | solution.py:47
  (141 shorter events, 152.3 us)
Async XLA Ops:
  0.6 69.8 %copy-start = (bf16[256,2048]{1,0:T(8,128)(2,1)S(1)}, bf16[256,2048]{1,0:T(8,128)(2,1)}, u32[]{:S(2)}) copy-start(bf16[256,2048]{1,0:T(8,128)(2,1)} %param.7) | copy-start | bytes 3145732
  64.8 5.6 copy-start.1
  606.5 27.6 %all-to-all-start.16 = ((bf16[16,128,128]{2,1,0:T(8,128)(2,1)}), bf16[16,128,128]{2,1,0:T(8,128)(2,1)S(1)}, u32[]{:S(2)}, u32[]{:S(2)}) async-start(bf16[16,128,128]{2,1,0:T(8,128)(2,1)} %bitcast.39), calls=%async_computation.16 | async-start | bytes 1048576 | tf_op jit(solution)/shard_map/all_to_all | solution.py:95
  635.0 12.7 %copy-start.2 = (s32[4]{0:T(128)S(1)}, s32[4]{0:T(128)}, u32[]{:S(2)}) copy-start(s32[4]{0:T(128)} %param.10) | copy-start | bytes 52
  635.0 44.3 %all-to-all-start.15 = ((f32[32,16,256]{2,1,0:T(8,128)}), f32[32,16,256]{2,1,0:T(8,128)S(1)}, u32[]{:S(2)}, u32[]{:S(2)}) async-start(f32[32,16,256]{2,1,0:T(8,128)} %broadcast_in_dim.37), calls=%async_computation.15 | async-start | bytes 1048576 | tf_op jit(solution)/shard_map/all_to_all | solution.py:47
